TPU v7x, 512 devices: a 8x2x16 block of a 8x16x16 slice. The times are simulated.
512 devices in a mesh: rep: 2 (over y), seq: 32 (over z, core), head: 8 (over x).
Axes of the slice: x: 8, y: 2, z: 16, core: 2. Of those that a mesh axis runs over, the one named last changes fastest.
The devices are a block of a 8x16x16 slice.
Arguments:
- queries: bfloat16 [16384, 4096], P(('rep', 'seq'), 'head'), parts along dimension 0, may hold values from -520 to 520
- rotated_key_states: bfloat16 [16384, 1024], P(('rep', 'seq'), 'head'), parts along dimension 0, may hold values from -6 to 6
- value_state_array: bfloat16 [16384, 1024], P(('rep', 'seq'), 'head'), parts along dimension 0, may hold values from -6 to 6
- residual: bfloat16 [16384, 4096], P(('rep', 'seq'), 'head'), parts along dimension 0, may hold values from -60 to 60
- out_weight: bfloat16 [4096, 4096], P('head'), may hold values from -0.75 to 0.75
- norm_gain: bfloat16 [4096], P('head'), may hold values from 0.5 to 1.5
- block_order: int32 [128], P('rep'), parts along dimension 0, may hold values from 0 to 63, as said below
Outputs:
- normed: bfloat16 [16384, 4096], P(('rep', 'seq'), 'head'), parts along dimension 0
There are 2 independent parts, one for each index of `rep`. A program takes and returns all parts, laid end to end along the dimension named above; an argument that names none is the same for every part. Nothing has to cross between parts.
Inputs may be any that keep to these rules, and one draw needn't show every extreme that they name: `block_order`: slots 2i and 2i + 1 hold blocks c and 63 - c in either order; every block appears once.
All inputs are finite; a program needn't handle non-finite values.
Results may differ from a plain program's by a relative error of at most 0.008.
Values may be sent and summed in bfloat16 or wider, within the bound.
A program may use at most 64 MiB of HBM per device.

v0:
```python
import math

import jax
import jax.numpy as jnp
from jax import lax
from jax.sharding import PartitionSpec as P

D = 4096
HEAD_SIZE = 128


norm_epsilon = 1e-05


def side_by_side(arrays, axis, dim, along):
    both = jnp.concatenate(arrays, axis=along)
    result, at, done = (lax.all_gather(both, axis, axis=dim, tiled=True), 0, [])
    for a in arrays:
        done.append(lax.slice_in_dim(result, at, at + a.shape[along], axis=along))
        at += a.shape[along]
    return tuple(done)


def copy_for_each(x, axis):
    copies = jnp.broadcast_to(x, (lax.axis_size(axis), *x.shape))
    return lax.all_to_all(copies, axis, split_axis=0, concat_axis=0, tiled=True)


def over_copies(x, axis):
    return copy_for_each(x, axis).sum(axis=0)


def slot_positions(row_ids, block_order, block_rows):
    slot_index = row_ids // block_rows
    slot_ids = jnp.arange(block_order.shape[0], dtype=jnp.int32)
    starts = jnp.sum(
        jnp.where(slot_index[:, None] == slot_ids[None, :], block_order[None, :], 0), axis=1
    )
    return starts * block_rows + row_ids % block_rows


def attend_block(carried, query_rows, query_positions, key_block, value_block, key_positions):
    row_peak, denominators, weighted_sum = carried
    scores = jnp.einsum(
        "qhgd,khd->hgqk", query_rows, key_block, preferred_element_type=jnp.float32
    ) * HEAD_SIZE ** (-0.5)
    visible = (key_positions[None, :] <= query_positions[:, None])[None, None]
    scores = jnp.where(visible, scores, -1e30)
    new_peak = jnp.maximum(row_peak, jnp.max(scores, axis=3))
    weights = jnp.where(visible, jnp.exp(scores - new_peak[..., None]), 0.0)
    factor = jnp.exp(row_peak - new_peak)
    denominators = denominators * factor + jnp.sum(weights, axis=3)
    weighted_sum = weighted_sum * factor[..., None] + jnp.einsum(
        "hgqk,khd->hgqd",
        weights.astype(jnp.bfloat16),
        value_block,
        preferred_element_type=jnp.float32,
    )
    return (new_peak, denominators, weighted_sum)


def body(
    queries, rotated_key_states, value_state_array, residual, out_weight, norm_gain, block_order
):
    tok_rows = queries.shape[0]
    block_rows = tok_rows // 2
    kv_heads = rotated_key_states.shape[1] // HEAD_SIZE
    heads_of_queries = queries.shape[1] // HEAD_SIZE
    queries_per_group = heads_of_queries // kv_heads
    own_rows = lax.axis_index("seq") * tok_rows + jnp.arange(tok_rows, dtype=jnp.int32)
    own_positions = slot_positions(own_rows, block_order, block_rows)
    shaped = queries.reshape(tok_rows, kv_heads, queries_per_group, HEAD_SIZE)
    query_sides = [
        (shaped[:block_rows], own_positions[:block_rows]),
        (shaped[block_rows:], own_positions[block_rows:]),
    ]

    def fresh_state():
        return (
            jnp.full((kv_heads, queries_per_group, block_rows), -1e30, jnp.float32),
            jnp.zeros((kv_heads, queries_per_group, block_rows), jnp.float32),
            jnp.zeros((kv_heads, queries_per_group, block_rows, HEAD_SIZE), jnp.float32),
        )

    key_piece, value_piece = side_by_side((rotated_key_states, value_state_array), "seq", 0, 1)
    piece_rows = key_piece.shape[0]
    width_rows = math.gcd(piece_rows, 512)
    heads_of_keys = key_piece.reshape(piece_rows, kv_heads, HEAD_SIZE)
    heads_of_values = value_piece.reshape(piece_rows, kv_heads, HEAD_SIZE)

    def one_step(block_index, states):
        offset = block_index * width_rows
        key_block = lax.dynamic_slice_in_dim(heads_of_keys, offset, width_rows, 0)
        value_block = lax.dynamic_slice_in_dim(heads_of_values, offset, width_rows, 0)
        row_ids = offset + jnp.arange(width_rows, dtype=jnp.int32)
        key_positions = slot_positions(row_ids, block_order, block_rows)
        updated = []
        for side_index in range(2):
            query_rows, query_positions = query_sides[side_index]
            updated.append(
                attend_block(
                    states[side_index],
                    query_rows,
                    query_positions,
                    key_block,
                    value_block,
                    key_positions,
                )
            )
        return tuple(updated)

    states = lax.fori_loop(0, piece_rows // width_rows, one_step, (fresh_state(), fresh_state()))
    outputs = []
    for side_state in states:
        row_peak, denominators, weighted_sum = side_state
        result = weighted_sum / denominators[..., None]
        outputs.append(
            result.transpose(2, 0, 1, 3).reshape(block_rows, heads_of_queries * HEAD_SIZE)
        )
    attention = jnp.concatenate(outputs, axis=0).astype(jnp.bfloat16)
    partial_terms = jnp.dot(attention, out_weight, preferred_element_type=jnp.float32)
    projected = lax.psum_scatter(
        partial_terms.astype(jnp.bfloat16), "head", scatter_dimension=1, tiled=True
    ).astype(jnp.float32)
    mixed_rows = residual.astype(jnp.float32) + projected
    squares = jnp.sum(mixed_rows * mixed_rows, axis=1)
    totals = over_copies(squares, "head")
    inverse = lax.rsqrt(totals / D + norm_epsilon)
    return (mixed_rows * inverse[:, None] * norm_gain.astype(jnp.float32)[None, :]).astype(
        jnp.bfloat16
    )


def solution(mesh):
    in_specs = (
        P(("rep", "seq"), "head"),
        P(("rep", "seq"), "head"),
        P(("rep", "seq"), "head"),
        P(("rep", "seq"), "head"),
        P("head", None),
        P("head"),
        P("rep"),
    )
    out_specs = P(("rep", "seq"), "head")
    return jax.shard_map(body, mesh=mesh, in_specs=in_specs, out_specs=out_specs, check_vma=False)
```

profile of v0, /device:TPU:80, one launch (start us, length us, event | category | flops | bytes accessed | tf_op | source)
XLA Modules:
  0.0 290.9 jit_solution(8093793578961961863)
XLA Ops:
  6.6 1.5 pad_maximum_fusion
  10.6 107.1 %all-gather.2.cloned.1.call-done = bf16[8192,256]{1,0:T(8,128)(2,1)} async-done(((bf16[256,256]{1,0:T(8,128)(2,1)}), bf16[8192,256]{1,0:T(8,128)(2,1)}) %all-gather.2.cloned.1.call-update) | async-done | bytes 4194320 | tf_op jit(solution)/shard_map/all_gather | solution.py:17
  117.8 4.5 %slice_bitcast_fusion = (bf16[8192,1,128]{2,0,1:T(8,128)(2,1)}, bf16[8192,1,128]{2,0,1:T(8,128)(2,1)}) fusion(bf16[8192,256]{1,0:T(8,128)(2,1)} %all-gather.2.cloned.1.call-done), kind=kLoop, calls=%fused_computation.68 | loop fusion | bytes 8388608 | tf_op jit(solution)/shard_map/reshape | solution.py:89
  122.2 95.4 %while.26 = (s32[]{:T(128)}, f32[1,4,128]{2,1,0:T(4,128)S(1)}, f32[1,4,128]{2,1,0:T(4,128)S(1)}, f32[1,4,128,128]{3,2,1,0:T(8,128)S(1)}, f32[1,4,128]{2,1,0:T(4,...) while((s32[]{:T(128)}, f32[1,4,128]{2,1,0:T(4,128)S(1)}, ...), condition=%wide.region_7.8_spmd.clone, body=%wide.region_1.7_spmd.clone.sunk | while | flops 273797632 | bytes 8730105 | solution.py:112
  123.8 1.3 fusion.78
  126.3 1.4 fusion.77
  132.3 1.3 fusion.77
  135.7 1.4 fusion.78
  138.3 1.3 fusion.77
  141.6 1.4 fusion.78
  147.6 1.4 fusion.78
  150.2 1.3 fusion.77
  153.6 1.4 fusion.78
  156.2 1.3 fusion.77
  159.5 1.4 fusion.78
  165.5 1.4 fusion.78
  171.4 1.4 fusion.78
  174.0 1.3 fusion.77
  177.4 1.4 fusion.78
  183.4 1.4 fusion.78
  189.3 1.4 fusion.78
  195.3 1.4 fusion.78
  197.9 1.3 fusion.77
  201.3 1.4 fusion.78
  207.2 1.4 fusion.78
  213.2 1.4 fusion.78
  215.8 1.3 fusion.77
  217.9 4.8 %convolution_convert_fusion = bf16[256,4096]{1,0:T(8,128)(2,1)} fusion(bf16[512,4096]{1,0:T(8,128)(2,1)} %param.13, bf16[128,512]{0,1:T(8,128)(2,1)S(1)} %bitcast.118, bf16[128,512]{0,1:T(8,128)(2,1)S(1)} %bitcast.117), kind=kOutput, calls=%fused_computation.67 | convolution fusion | flops 1075314688 | bytes 6553600 | tf_op jit(solution)/shard_map/dot_general | solution.py:121
  222.8 45.5 %reduce-scatter.2.cloned.1.call-done = bf16[256,512]{1,0:T(8,128)(2,1)} async-done(((bf16[256,4096]{1,0:T(8,128)(2,1)}), bf16[256,512]{1,0:T(8,128)(2,1)}) %reduce-scatter.2.cloned.1.call-update) | async-done | bytes 262160 | tf_op jit(solution)/shard_map/reduce_scatter | solution.py:122
  270.0 4.5 %all-to-all-start = ((f32[8,1,256]{2,1,0:T(1,128)}), f32[8,1,256]{2,1,0:T(1,128)S(1)}, u32[]{:S(2)}, u32[]{:S(2)}) async-start(f32[8,1,256]{2,1,0:T(1,128)} %broadcast_in_dim.155), calls=%async_computation.1 | async-start | bytes 16384 | tf_op jit(solution)/shard_map/all_to_all | solution.py:26
  274.5 7.7 %all-to-all-done = f32[8,1,256]{2,1,0:T(1,128)S(1)} async-done(((f32[8,1,256]{2,1,0:T(1,128)}), f32[8,1,256]{2,1,0:T(1,128)S(1)}, u32[]{:S(2)}, u32[]{:S(2)}) %all-to-all-start) | async-done | bytes 8224 | tf_op jit(solution)/shard_map/all_to_all | solution.py:26
  282.3 1.8 multiply_convert_fusion
  (251 shorter events, 67.3 us)
Async XLA Ops:
  6.5 111.2 %all-gather.2.cloned.1.call-start = ((), (), s32[]{:S(2)}) async-start(), calls=%async_computation.2 | async-start | bytes 4325376 | tf_op jit(solution)/shard_map/all_gather | solution.py:17
  8.2 260.1 %reduce-scatter.2.cloned.1.call-start = ((), (), s32[]{:S(2)}) async-start(), calls=%async_computation.3 | async-start | bytes 2359296 | tf_op jit(solution)/shard_map/reduce_scatter | solution.py:122
  10.6 111.6 %copy-start.1 = (s32[64]{0:T(128)S(1)}, s32[64]{0:T(128)}, u32[]{:S(2)}) copy-start(s32[64]{0:T(128)} %param.15) | copy-start | bytes 772
  222.8 45.5 %copy-start = (bf16[256,512]{1,0:T(8,128)(2,1)S(1)}, bf16[256,512]{1,0:T(8,128)(2,1)}, u32[]{:S(2)}) copy-start(bf16[256,512]{1,0:T(8,128)(2,1)} %param.12) | copy-start | bytes 786436
  222.8 51.7 %copy-start.2 = (bf16[512]{0:T(512)(128)(2,1)S(1)}, bf16[512]{0:T(512)(128)(2,1)}, u32[]{:S(2)}) copy-start(bf16[512]{0:T(512)(128)(2,1)} %param.14) | copy-start | bytes 3076
  270.0 12.2 %all-to-all-start = ((f32[8,1,256]{2,1,0:T(1,128)}), f32[8,1,256]{2,1,0:T(1,128)S(1)}, u32[]{:S(2)}, u32[]{:S(2)}) async-start(f32[8,1,256]{2,1,0:T(1,128)} %broadcast_in_dim.155), calls=%async_computation.1 | async-start | bytes 16384 | tf_op jit(solution)/shard_map/all_to_all | solution.py:26
Sparse Core Ops, SparseCore 0:
  9.5 108.2 all-gather.1
  223.0 45.2 reduce-scatter.1
where the time goes:
time: 292 us; the launch traced here: 291 us
  waiting for transfers between devices  160 us (55%)
  matrix products  87.1 us (30%)
  other arithmetic  16.8 us (6%)
  between operations  13.6 us (5%)
  local copies, waits for them, and re-layouts  6.93 us (2%)
  starting transfers between devices  4.54 us (2%)
    all_gather x1, waiting for transfers between devices, side_by_side(): result, at, done = (lax.all_gather(both, axis, axis=dim, tiled=True), 0, [])  107 us
    reduce_scatter x1, waiting for transfers between devices, body(): lax.psum_scatter(partial_terms.astype(jnp.bfloat16), 'head', scatter_dime...  45.5 us
    dot_general x32, matrix products, attend_block(): jnp.einsum('hgqk,khd->hgqd', weights.astype(jnp.bfloat16), value_block, p...  43.2 us
    dot_general x32, matrix products, attend_block(): jnp.einsum('qhgd,khd->hgqk', query_rows, key_block, preferred_element_typ...  39.1 us
    all_to_all x1, waiting for transfers between devices, copy_for_each(): return lax.all_to_all(copies, axis, split_axis=0, concat_axis=0, tiled=True)  7.71 us
    reduce_sum x32, other arithmetic, attend_block(): denominators = denominators * factor + jnp.sum(weights, axis=3)  6.64 us
  transfers between devices with their start and end apart: 3, of which 3 were waited for; matrix products, arithmetic and copies ran while one was open for 1% of the time, Pallas kernels for 0%

commit v1 on v0

v1 whole, which is shorter than its diff:
```python
import functools
import math

import jax
import jax.numpy as jnp
from jax import lax
from jax.experimental import pallas as pl
from jax.experimental.pallas import tpu as pltpu
from jax.sharding import PartitionSpec as P

HEAD_SIZE = 128
NORM_EPSILON = 1e-05
BIG = 1e30
MESH = pl.DeviceIdType.MESH
F32 = jnp.float32
BF16 = jnp.bfloat16
SCALE = math.log2(math.e) * HEAD_SIZE ** (-0.5)
RELAY = 1


def kernel(
    dims,
    order_ref, q_ref, k_ref, v_ref, res_ref, w_hbm, gain_ref,
    out_ref,
    wv, qs, kbuf, vbuf, acc, peak, att, xs, xr, mixed, ssq_out, ssq_in,
    wsem, pair_send, pair_recv, ring_send, ring_recv, share_send, xs_sem, xr_sem, n_send, n_recv,
):
    nz, nx, heads, block = dims
    half_z = nz // 2
    rows = heads * block
    width = res_ref.shape[1]
    half = width // 2
    me = lax.axis_index("seq")
    core = lax.rem(me, 2)
    z = me // 2
    hx = lax.axis_index("head")
    sib = z * 2 + 1 - core
    zr = lax.rem(z + 1, nz) * 2 + core
    zl = lax.rem(z + nz - 1, nz) * 2 + core

    w_copy = pltpu.make_async_copy(w_hbm, wv, wsem)
    w_copy.start()

    barrier = pltpu.get_barrier_semaphore()
    for target in (sib, zr, zl):
        pl.semaphore_signal(barrier, inc=1, device_id={"seq": target}, device_id_type=MESH)
    for d in range(1, nx):
        pl.semaphore_signal(
            barrier, inc=1, device_id={"head": lax.rem(hx + d, nx)}, device_id_type=MESH
        )

    swapped = order_ref[2 * me] > order_ref[2 * me + 1]

    def pick(g, ref, cols):
        top, bottom = ref[pl.ds(0, block), cols], ref[pl.ds(block, block), cols]
        return lax.select_n(swapped, *((top, bottom) if g == 0 else (bottom, top)))

    every = slice(None)
    own_half = pl.ds(pl.multiple_of(core * block, block), block)
    sib_half = pl.ds(pl.multiple_of((1 - core) * block, block), block)
    for g in range(2):
        kbuf[g, 0, 0, own_half, :] = pick(g, k_ref, every)
        vbuf[g, 0, 0, own_half, :] = pick(g, v_ref, every)
    bufs = (kbuf, vbuf)

    pl.semaphore_wait(barrier, 2 + nx)

    def pair_copy(g, t):
        return pltpu.make_async_remote_copy(
            src_ref=bufs[t].at[g, 0, 0, own_half, :],
            dst_ref=bufs[t].at[g, 0, 0, own_half, :],
            send_sem=pair_send.at[g, t],
            recv_sem=pair_recv.at[g, t],
            device_id={"seq": sib},
            device_id_type=MESH,
        )

    def ring_copy(g, t, s, d):
        source = bufs[t].at[g, 0, 0] if isinstance(s, int) and s == 0 else bufs[t].at[g, s, d]
        return pltpu.make_async_remote_copy(
            src_ref=source,
            dst_ref=bufs[t].at[g, s + 1, d],
            send_sem=ring_send.at[g, t, s, d],
            recv_sem=ring_recv.at[g, t, s + 1, d],
            device_id={"seq": (zr, zl)[d]},
            device_id_type=MESH,
        )

    def share_copy(g, t, s, d):
        return pltpu.make_async_remote_copy(
            src_ref=bufs[t].at[g, s, d],
            dst_ref=bufs[t].at[g, s, d],
            send_sem=share_send.at[g, t, s, d],
            recv_sem=ring_recv.at[g, t, s, d],
            device_id={"seq": sib},
            device_id_type=MESH,
        )

    def wait_arrival(g, t, s, d):
        pltpu.make_async_copy(
            bufs[t].at[g, s, d], bufs[t].at[g, s, d], ring_recv.at[g, t, s, d]
        ).wait()

    for g in range(2):
        for t in range(2):
            pair_copy(g, t).start()

    for g in range(2):
        for h in range(heads):
            qs[pl.ds(g * rows + h * block, block), :] = pick(
                g, q_ref, pl.ds(h * HEAD_SIZE, HEAD_SIZE)
            )
    peak[...] = jnp.full_like(peak, -BIG)
    acc[...] = jnp.zeros_like(acc)

    for g in range(2):
        for t in range(2):
            pltpu.make_async_copy(
                bufs[t].at[g, 0, 0, sib_half, :],
                bufs[t].at[g, 0, 0, sib_half, :],
                pair_recv.at[g, t],
            ).wait()

            @pl.when(core == RELAY)
            def _(g=g, t=t):
                ring_copy(g, t, 0, 0).start()
                ring_copy(g, t, 0, 1).start()

    def low_of(index):
        a, b = order_ref[2 * index], order_ref[2 * index + 1]
        return jnp.minimum(a, b)

    my_low = low_of(me)

    def hidden(g, index):
        lo = low_of(index)
        seen = (lo < my_low) if g == 0 else (lo > my_low)
        return jnp.where(seen, F32(0.0), F32(BIG))

    tile_rows = min(rows, 256)

    def flash(qg, kc, vc, masks):
        keys = kc.shape[0]
        spans = keys // block
        vext = jnp.concatenate([vc, jnp.ones_like(vc)], axis=1)
        for i in range(rows // tile_rows):
            r = pl.ds(qg * rows + i * tile_rows, tile_rows)
            scores = lax.dot_general(
                qs[r, :], kc, (((1,), (1,)), ((), ())), preferred_element_type=F32
            )
            old = peak[r, :]
            parts = [scores[:, b * block:(b + 1) * block] for b in range(spans)]
            if masks is not None:
                parts = [p if m is None else p - m for p, m in zip(parts, masks)]
            best = functools.reduce(jnp.maximum, parts)
            new = jnp.maximum(old, jnp.max(best, axis=1, keepdims=True))
            weights = jnp.concatenate(
                [jnp.exp2((p - new) * SCALE).astype(BF16) for p in parts], axis=1
            )
            factor = jnp.exp2((old - new) * SCALE)
            peak[r, :] = new
            part = jnp.dot(weights, vext, preferred_element_type=F32)
            acc[r, :] = acc[r, :] * jnp.concatenate([factor, factor], axis=1) + part

    row_id = lax.broadcasted_iota(jnp.int32, (tile_rows, block), 0)
    col_id = lax.broadcasted_iota(jnp.int32, (tile_rows, block), 1)
    triangle = jnp.where(col_id <= lax.rem(row_id, block), F32(0.0), F32(BIG))

    def own_chunk(g, t):
        return jnp.concatenate(
            [bufs[t][g, 0, 0, own_half, :], bufs[t][g, 0, 0, sib_half, :]], axis=0
        )

    low_k, low_v = own_chunk(0, 0), own_chunk(0, 1)
    flash(0, low_k, low_v, [triangle, hidden(0, sib)])
    flash(1, low_k, low_v, None)

    def chunk(g, t, s):
        return jnp.concatenate([bufs[t][g, s, 0], bufs[t][g, s, 1]], axis=0)

    def masks_of(g, s):
        left = lax.rem(z + nz - s, nz)
        right = lax.rem(z + s, nz)
        return [
            hidden(g, 2 * left), hidden(g, 2 * left + 1),
            hidden(g, 2 * right), hidden(g, 2 * right + 1),
        ]

    def receive(g, t, s, last):
        for d in range(2):
            wait_arrival(g, t, s, d)

            @pl.when(core == RELAY)
            def _(d=d):
                if not last or d == t:
                    ring_copy(g, t, s, d).start()
                share_copy(g, t, s, d).start()

    def high_own():
        flash(1, own_chunk(1, 0), own_chunk(1, 1), [triangle, hidden(1, sib)])

    def step(s, last, before):
        receive(0, 0, s, last)
        before()
        receive(0, 1, s, last)
        flash(0, chunk(0, 0, s), chunk(0, 1, s), masks_of(0, s))
        receive(1, 0, s, last)
        flash(1, chunk(0, 0, s), chunk(0, 1, s), None)
        receive(1, 1, s, last)

    def high_step(s):
        flash(1, chunk(1, 0, s), chunk(1, 1, s), masks_of(1, s))

    step(1, half_z == 2, high_own)

    def loop_body(s, carry):
        step(s, False, lambda: high_step(s - 1))
        return carry

    lax.fori_loop(2, half_z - 1, loop_body, 0)
    if half_z > 2:
        step(half_z - 1, True, lambda: high_step(half_z - 2))

    far = lax.rem(z + half_z, nz)

    def receive_last(g, t):
        wait_arrival(g, t, half_z, t)

        @pl.when(core == RELAY)
        def _():
            share_copy(g, t, half_z, t).start()

    def far_masks(g):
        return [hidden(g, 2 * far), hidden(g, 2 * far + 1)]

    def finish(g):
        for h in range(heads):
            r = pl.ds(g * rows + h * block, block)
            att[g, :, pl.ds(h * HEAD_SIZE, HEAD_SIZE)] = (
                acc[r, pl.ds(0, HEAD_SIZE)] / acc[r, pl.ds(HEAD_SIZE, HEAD_SIZE)]
            ).astype(BF16)

    def project(g, owner):
        return jnp.dot(
            att[g],
            wv[:, pl.ds(pl.multiple_of(owner * width, width), width)],
            preferred_element_type=F32,
        )

    def x_copy(g, d, o, p):
        return pltpu.make_async_remote_copy(
            src_ref=xs.at[g, d, o - 1, p],
            dst_ref=xr.at[g, d, o - 1, p],
            send_sem=xs_sem.at[g, d, o - 1, p],
            recv_sem=xr_sem.at[g, d, o - 1, p],
            device_id={"head": lax.rem(hx + (1, nx - 1)[d], nx)},
            device_id_type=MESH,
        )

    half_x = nx // 2
    halves = (pl.ds(0, half), pl.ds(half, half))

    def reduce_stage(g, o):
        if o == half_x:
            own = project(g, lax.rem(hx + o, nx)).astype(BF16)
            for d in range(2):
                xs[g, d, o - 1, d] = own[:, d * half:(d + 1) * half]
                x_copy(g, d, o, d).start()
            return
        for d in range(2):
            own = project(g, lax.rem(hx + (o, nx - o)[d], nx))
            for p in (1 - d, d):
                term = own[:, p * half:(p + 1) * half]
                if o + 1 < half_x or p == d:
                    x_copy(g, d, o + 1, p).wait_recv()
                    term = term + xr[g, d, o, p].astype(F32)
                xs[g, d, o - 1, p] = term.astype(BF16)
                x_copy(g, d, o, p).start()

    def norm_copy(g, d):
        return pltpu.make_async_remote_copy(
            src_ref=ssq_out.at[g],
            dst_ref=ssq_in.at[g, d - 1],
            send_sem=n_send.at[g, d - 1],
            recv_sem=n_recv.at[g, d - 1],
            device_id={"head": lax.rem(hx + d, nx)},
            device_id_type=MESH,
        )

    def reduce_last(g):
        total = project(g, hx) + pick(g, res_ref, every).astype(F32)
        sides = []
        for p in range(2):
            side = total[:, p * half:(p + 1) * half]
            for d in (1 - p, p):
                x_copy(g, d, 1, p).wait_recv()
                side = side + xr[g, d, 0, p].astype(F32)
            mixed[g, :, halves[p]] = side
            sides.append(side)
        squares = sides[0] * sides[0] + sides[1] * sides[1]
        pieces = [squares[:, c * block:(c + 1) * block] for c in range(half // block)]
        column = functools.reduce(jnp.add, pieces)
        row = jnp.sum(column.T, axis=0, keepdims=True)
        ssq_out[g] = jnp.broadcast_to(row, ssq_out.shape[1:])
        for d in range(1, nx):
            norm_copy(g, d).start()

    def output(g):
        total = ssq_out[g]
        for d in range(1, nx):
            norm_copy(g, d).wait_recv()
            total = total + ssq_in[g, d - 1]
        inverse = lax.rsqrt(total / (nx * width) + NORM_EPSILON)
        column = jnp.broadcast_to(inverse[0:1, :], (block, block)).T
        for c in range(width // block):
            cols = pl.ds(c * block, block)
            out_ref[g, :, cols] = (
                mixed[g, :, cols] * column * gain_ref[:, cols].astype(F32)
            ).astype(BF16)

    receive_last(0, 0)
    high_step(half_z - 1)
    receive_last(0, 1)
    low_k, low_v = bufs[0][0, half_z, 0], bufs[1][0, half_z, 1]
    flash(0, low_k, low_v, far_masks(0))
    finish(0)
    w_copy.wait()
    reduce_stage(0, half_x)
    flash(1, low_k, low_v, None)
    receive_last(1, 0)
    receive_last(1, 1)
    flash(1, bufs[0][1, half_z, 0], bufs[1][1, half_z, 1], far_masks(1))
    finish(1)
    reduce_stage(1, half_x)
    for o in range(half_x - 1, 0, -1):
        for g in range(2):
            reduce_stage(g, o)
    reduce_last(0)
    reduce_last(1)
    output(0)
    output(1)

    for g in range(2):
        for t in range(2):
            pair_copy(g, t).wait_send()
        for d in range(1, nx):
            norm_copy(g, d).wait_send()
        for d in range(2):
            for o in range(1, half_x + 1):
                for p in range(2):
                    if o < half_x or p == d:
                        x_copy(g, d, o, p).wait_send()

    @pl.when(core == RELAY)
    def _():
        for g in range(2):
            for t in range(2):
                for d in range(2):
                    ring_copy(g, t, 0, d).wait_send()
                    if d == t:
                        ring_copy(g, t, half_z - 1, d).wait_send()
                        share_copy(g, t, half_z, d).wait_send()
                    share_copy(g, t, half_z - 1, d).wait_send()

        def drain(s, carry):
            for g in range(2):
                for t in range(2):
                    for d in range(2):
                        ring_copy(g, t, s, d).wait_send()
                        share_copy(g, t, s, d).wait_send()
            return carry

        lax.fori_loop(1, half_z - 1, drain, 0)


def body(queries, keys, values, residual, out_weight, norm_gain, block_order):
    nz = lax.axis_size("seq") // 2
    nx = lax.axis_size("head")
    tokens, q_width = queries.shape
    block = tokens // 2
    heads = q_width // HEAD_SIZE
    width = residual.shape[1]
    rows = heads * block
    half_z, half_x = nz // 2, nx // 2
    vmem = pl.BlockSpec(memory_space=pltpu.VMEM)
    dma = pltpu.SemaphoreType.DMA
    result = pl.pallas_call(
        functools.partial(kernel, (nz, nx, heads, block)),
        out_shape=jax.ShapeDtypeStruct((2, block, width), BF16),
        in_specs=[
            pl.BlockSpec(memory_space=pltpu.SMEM), vmem, vmem, vmem, vmem,
            pl.BlockSpec(memory_space=pl.ANY), vmem,
        ],
        out_specs=vmem,
        scratch_shapes=[
            pltpu.VMEM(out_weight.shape, BF16),
            pltpu.VMEM((2 * rows, HEAD_SIZE), BF16),
            pltpu.VMEM((2, half_z + 1, 2, tokens, HEAD_SIZE), BF16),
            pltpu.VMEM((2, half_z + 1, 2, tokens, HEAD_SIZE), BF16),
            pltpu.VMEM((2 * rows, 2 * HEAD_SIZE), F32),
            pltpu.VMEM((2 * rows, block), F32),
            pltpu.VMEM((2, block, q_width), BF16),
            pltpu.VMEM((2, 2, half_x, 2, block, width // 2), BF16),
            pltpu.VMEM((2, 2, half_x, 2, block, width // 2), BF16),
            pltpu.VMEM((2, block, width), F32),
            pltpu.VMEM((2, 8, block), F32),
            pltpu.VMEM((2, nx - 1, 8, block), F32),
            dma,
            dma((2, 2)),
            dma((2, 2)),
            dma((2, 2, half_z, 2)),
            dma((2, 2, half_z + 1, 2)),
            dma((2, 2, half_z + 1, 2)),
            dma((2, 2, half_x, 2)),
            dma((2, 2, half_x, 2)),
            dma((2, nx - 1)),
            dma((2, nx - 1)),
        ],
        compiler_params=pltpu.CompilerParams(
            collective_id=0, has_side_effects=True, vmem_limit_bytes=40 * 1024 * 1024
        ),
    )(
        block_order, queries, keys, values, residual, out_weight,
        norm_gain.reshape(1, width),
    )
    me = lax.axis_index("seq")
    pair = lax.dynamic_slice_in_dim(block_order, 2 * me, 2)
    swapped = pair[0] > pair[1]
    first = jnp.where(swapped, result[1], result[0])
    second = jnp.where(swapped, result[0], result[1])
    return jnp.concatenate([first, second], axis=0)


def solution(mesh):
    split = P(("rep", "seq"), "head")
    return jax.shard_map(
        body,
        mesh=mesh,
        in_specs=(split, split, split, split, P("head", None), P("head"), P("rep")),
        out_specs=split,
        check_vma=False,
    )
```

time: 292 us -> 115 us (0.39)
  waiting for transfers between devices: 160 us -> 0 us
  Pallas kernels: 0 us -> 105 us
  matrix products: 87.1 us -> 0 us
  other arithmetic: 16.8 us -> 0.74 us
  between operations: 13.6 us -> 1.24 us
  starting transfers between devices: 4.54 us -> 0 us
    all_gather x1 -> x0, waiting for transfers between devices: 107 us -> none  [side_by_side(): result, at, done = (lax.all_gather(both, axis, axis=dim, tiled=True), 0, [])]
    pallas_call x0 -> x1, Pallas kernels: none -> 105 us  [body(): pl.pallas_call(functools.partial(kernel, (nz, nx, heads, block)), out_sha...]
    dot_general x65 -> x0, matrix products: 87.1 us -> none  [the longest x32 43.2 us: attend_block(): jnp.einsum('hgqk,khd->hgqd', weights.astype(jnp.bfloat16), value_block, p...]
    reduce_scatter x1 -> x0, waiting for transfers between devices: 45.5 us -> none  [body(): lax.psum_scatter(partial_terms.astype(jnp.bfloat16), 'head', scatter_dime...]
    reduce_sum x51 -> x0, other arithmetic: 10.1 us -> none  [the longest x32 6.64 us: attend_block(): denominators = denominators * factor + jnp.sum(weights, axis=3)]
    all_to_all x1 -> x0, waiting for transfers between devices: 7.71 us -> none  [copy_for_each(): return lax.all_to_all(copies, axis, split_axis=0, concat_axis=0, tiled=True)]
    unnamed x10 -> x12, local copies, waits for them, and re-layouts: 0.52 us -> 6.42 us
    all_to_all x1 -> x0, starting transfers between devices: 4.47 us -> none  [copy_for_each(): return lax.all_to_all(copies, axis, split_axis=0, concat_axis=0, tiled=True)]
  transfers between devices with their start and end apart: 3 -> 0, of which waited for: 3 -> 0; matrix products, arithmetic and copies ran while one was open for 1% -> 0% of each run, Pallas kernels for 0% -> 0%
where the time goes in v1:
time: 115 us
  Pallas kernels  105 us (91%)
  local copies, waits for them, and re-layouts  8.42 us (7%)
  between operations  1.24 us (1%)
    pallas_call x1, Pallas kernels, body(): pl.pallas_call(functools.partial(kernel, (nz, nx, heads, block)), out_sha...  105 us
    unnamed x12, local copies, waits for them, and re-layouts  6.42 us

profile of v1, /device:TPU:80, one launch (start us, length us, event | category | flops | bytes accessed | tf_op | source)
XLA Modules:
  0.0 115.0 jit_solution(651650960124306319)
XLA Ops:
  0.0 0.7 dynamic_slice.3
  0.7 0.6 fusion
  2.5 0.7 reshape.8.gain_ref
  3.2 0.0 copy-start
  3.2 2.2 %copy-done = bf16[512,4096]{1,0:T(8,128)(2,1)S(1)} copy-done((bf16[512,4096]{1,0:T(8,128)(2,1)S(1)}, bf16[512,4096]{1,0:T(8,128)(2,1)}, u32[]{:S(2)}) %copy-start) | copy-done | bytes 4194328
  5.4 0.0 copy-start.1
  5.4 0.9 copy-done.1
  6.4 0.0 copy-start.2
  6.4 0.9 copy-done.2
  7.3 0.0 copy-start.3
  7.3 0.8 copy-done.3
  8.1 0.0 copy-start.4
  8.1 0.8 copy-done.4
  9.0 0.0 copy-start.5
  9.0 0.7 copy-done.5
  9.6 104.6 %shard_map.73 = bf16[2,128,512]{2,1,0:T(8,128)(2,1)S(1)} custom-call(s32[64]{0:T(128)S(1)} %copy-done.5, bf16[256,512]{1,0:T(8,128)(2,1)S(1)} %copy-done.1, bf16[256,128]{1,0:T(8,128)(2,1)S(1)} %copy-done.3, bf16[256,128]{1,0:T(8,128)(2,1)S(1)} %copy-done.4, bf16[256,512]{1,0:T(8,128)(2,1)S(1)} %copy-done.2, bf16[512,4096]{1,0:T(8,128)(2,1)S(1)} %copy-done, ...), custom_call_target="tpu_custom_call" | custom-call | tf_op jit(solution)/shard_map/pallas_call | solution.py:387
  114.3 0.7 pad_maximum_fusion
  (1 shorter events, 0.0 us)
Async XLA Ops:
  3.2 2.2 %copy-start = (bf16[512,4096]{1,0:T(8,128)(2,1)S(1)}, bf16[512,4096]{1,0:T(8,128)(2,1)}, u32[]{:S(2)}) copy-start(bf16[512,4096]{1,0:T(8,128)(2,1)} %w_hbm.1) | copy-start | bytes 12582916
  5.4 0.9 copy-start.1
  6.4 0.9 copy-start.2
  7.3 0.8 copy-start.3
  8.1 0.8 copy-start.4
  9.0 0.7 copy-start.5

commit v2 on v1

v2 whole, which is shorter than its diff:
```python
import functools
import math

import jax
import jax.numpy as jnp
from jax import lax
from jax.experimental import pallas as pl
from jax.experimental.pallas import tpu as pltpu
from jax.sharding import PartitionSpec as P

HEAD_SIZE = 128
NORM_EPSILON = 1e-05
BIG = 1e30
MESH = pl.DeviceIdType.MESH
F32 = jnp.float32
BF16 = jnp.bfloat16
SCALE = math.log2(math.e) * HEAD_SIZE ** (-0.5)


LAG = 4


def kernel(
    dims,
    order_hbm, q_hbm, k_hbm, v_hbm, res_hbm, w_hbm,
    out_ref,
    order_ref, q_in, k_in, v_in, res_ref, wv, qs, kv, acc, peak, att, xs, xr, mixed, ssq_out, ssq_in,
    in_sem, pair_send, pair_recv, ring_send, ring_recv, share_send, xs_sem, xr_sem, n_send, n_recv,
):
    nz, nx, heads, block = dims
    half_z, half_x = nz // 2, nx // 2
    rows = heads * block
    width = res_ref.shape[1]
    half = width // 2
    me = lax.axis_index("seq")
    core = lax.rem(me, 2)
    z = me // 2
    hx = lax.axis_index("head")
    sib = z * 2 + 1 - core
    heading = 2 * core - 1
    mine, other = 1 - core, core
    ahead = lax.rem(z + heading + nz, nz) * 2 + core
    behind = lax.rem(z - heading + nz, nz) * 2 + core
    early = z < half_z

    loads = [
        pltpu.make_async_copy(a, b, in_sem.at[i])
        for i, (a, b) in enumerate(
            [(k_hbm, k_in), (v_hbm, v_in), (order_hbm, order_ref), (q_hbm, q_in),
             (res_hbm, res_ref), (w_hbm, wv)]
        )
    ]
    for load in loads:
        load.start()

    barrier = pltpu.get_barrier_semaphore()
    for target in (behind, sib):
        pl.semaphore_signal(barrier, inc=1, device_id={"seq": target}, device_id_type=MESH)
    for d in range(1, nx):
        pl.semaphore_signal(
            barrier, inc=1, device_id={"head": lax.rem(hx + d, nx)}, device_id_type=MESH
        )

    for load in loads[:3]:
        load.wait()
    swapped = order_ref[2 * me] > order_ref[2 * me + 1]

    def pick(g, ref, cols):
        top, bottom = ref[pl.ds(0, block), cols], ref[pl.ds(block, block), cols]
        return lax.select_n(swapped, *((top, bottom) if g == 0 else (bottom, top)))

    every = slice(None)
    own_half = pl.ds(pl.multiple_of(core * block, block), block)
    sib_half = pl.ds(pl.multiple_of((1 - core) * block, block), block)
    for g in range(2):
        for t, ref in enumerate((k_in, v_in)):
            kv[g, t, 0, 0, own_half, :] = pick(g, ref, every)

    pl.semaphore_wait(barrier, 1 + nx)

    def pair_copy(g, t):
        return pltpu.make_async_remote_copy(
            src_ref=kv.at[g, t, 0, 0, own_half, :],
            dst_ref=kv.at[g, t, 0, 0, own_half, :],
            send_sem=pair_send.at[g, t],
            recv_sem=pair_recv.at[g, t],
            device_id={"seq": sib},
            device_id_type=MESH,
        )

    def ring_copy(g, t, s):
        source = kv.at[g, t, 0, 0] if isinstance(s, int) and s == 0 else kv.at[g, t, s, mine]
        return pltpu.make_async_remote_copy(
            src_ref=source,
            dst_ref=kv.at[g, t, s + 1, mine],
            send_sem=ring_send.at[g, t, s],
            recv_sem=ring_recv.at[g, t, s + 1, mine],
            device_id={"seq": ahead},
            device_id_type=MESH,
        )

    def share_copy(g, t, s):
        return pltpu.make_async_remote_copy(
            src_ref=kv.at[g, t, s, mine],
            dst_ref=kv.at[g, t, s, mine],
            send_sem=share_send.at[g, t, s],
            recv_sem=ring_recv.at[g, t, s, mine],
            device_id={"seq": sib},
            device_id_type=MESH,
        )

    def arrived(g, t, s, d):
        piece = kv.at[g, t, s, d]
        pltpu.make_async_copy(piece, piece, ring_recv.at[g, t, s, d]).wait()

    def pair_arrived(g):
        for t in range(2):
            piece = kv.at[g, t, 0, 0, sib_half, :]
            pltpu.make_async_copy(piece, piece, pair_recv.at[g, t]).wait()

    for g in range(2):
        for t in range(2):
            pair_copy(g, t).start()

    def low_of(index):
        return jnp.minimum(order_ref[2 * index], order_ref[2 * index + 1])

    my_low = low_of(me)

    def hidden(g, plane):
        masks = []
        for c in range(2):
            lo = low_of(2 * plane + c)
            seen = (lo < my_low) if g == 0 else (lo > my_low)
            masks.append(jnp.where(seen, F32(0.0), F32(BIG)))
        return masks

    def hidden_sib(g):
        lo = low_of(sib)
        seen = (lo < my_low) if g == 0 else (lo > my_low)
        return jnp.where(seen, F32(0.0), F32(BIG))

    tile_rows = min(rows, 256)

    def flash(qg, kc, vc, masks):
        keys = kc.shape[0]
        spans = keys // block
        vext = jnp.concatenate([vc, jnp.ones_like(vc)], axis=1)
        for i in range(rows // tile_rows):
            r = pl.ds(qg * rows + i * tile_rows, tile_rows)
            scores = lax.dot_general(
                qs[r, :], kc, (((1,), (1,)), ((), ())), preferred_element_type=F32
            )
            old = peak[r, :]
            parts = [scores[:, b * block:(b + 1) * block] for b in range(spans)]
            if masks is not None:
                parts = [p - m for p, m in zip(parts, masks)]
            best = functools.reduce(jnp.maximum, parts)
            new = jnp.maximum(old, jnp.max(best, axis=1, keepdims=True))
            weights = jnp.concatenate(
                [jnp.exp2((p - new) * SCALE).astype(BF16) for p in parts], axis=1
            )
            factor = jnp.exp2((old - new) * SCALE)
            peak[r, :] = new
            part = jnp.dot(weights, vext, preferred_element_type=F32)
            acc[r, :] = acc[r, :] * jnp.concatenate([factor, factor], axis=1) + part

    def own_chunk(g, t):
        return jnp.concatenate(
            [kv[g, t, 0, 0, own_half, :], kv[g, t, 0, 0, sib_half, :]], axis=0
        )

    def plane_of(s, sign):
        return lax.rem(z + sign * s + nz, nz)

    def low_single(s, d, sign):
        flash(0, kv[0, 0, s, d], kv[0, 1, s, d], hidden(0, plane_of(s, sign)))

    def both(g, t, s):
        return jnp.concatenate([kv[g, t, s, 0], kv[g, t, s, 1]], axis=0)

    def relay(g, s, last):
        for t in range(2):
            arrived(g, t, s, mine)
            if not last:
                ring_copy(g, t, s).start()
            share_copy(g, t, s).start()
        if last:
            ring_copy(g, mine, s).start()

    def relay_far(g):
        arrived(g, mine, half_z, mine)
        share_copy(g, mine, half_z).start()

    loads[3].wait()
    for g in range(2):
        for h in range(heads):
            qs[pl.ds(g * rows + h * block, block), :] = pick(
                g, q_in, pl.ds(h * HEAD_SIZE, HEAD_SIZE)
            )
    peak[...] = jnp.full_like(peak, -BIG)
    acc[...] = jnp.zeros_like(acc)

    pair_arrived(0)
    for t in range(2):
        ring_copy(0, t, 0).start()
    pair_arrived(1)

    @pl.when(core == 0)
    def _():
        for t in range(2):
            ring_copy(1, t, 0).start()

    row_id = lax.broadcasted_iota(jnp.int32, (tile_rows, block), 0)
    col_id = lax.broadcasted_iota(jnp.int32, (tile_rows, block), 1)
    triangle = jnp.where(col_id <= lax.rem(row_id, block), F32(0.0), F32(BIG))

    low_k, low_v = own_chunk(0, 0), own_chunk(0, 1)
    flash(0, low_k, low_v, [triangle, hidden_sib(0)])
    flash(1, low_k, low_v, None)
    flash(1, own_chunk(1, 0), own_chunk(1, 1), [triangle, hidden_sib(1)])

    def other_low(s):
        for t in range(2):
            arrived(0, t, s, other)
        low_single(s, other, heading)

    last_step = half_z - 1
    lag = min(LAG, last_step - 1)

    def low_step(s, last, lagged):
        relay(0, s, last)
        low_single(s, mine, -heading)
        if lagged:
            other_low(s - lag)

        @pl.when(core == 0)
        def _():
            relay(1, s, last)

    def loop(first, stop, step):
        def body_of(s, carry):
            step(s)
            return carry

        lax.fori_loop(first, stop, body_of, 0)

    loop(1, lag + 1, lambda s: low_step(s, False, False))
    loop(lag + 1, last_step, lambda s: low_step(s, False, True))
    low_step(last_step, True, True)
    relay_far(0)

    @pl.when(core == 0)
    def _():
        relay_far(1)

    def high_relays():
        loop(1, last_step, lambda s: relay(1, s, False))
        relay(1, last_step, True)
        relay_far(1)

    @pl.when(core == 1)
    def _():
        for t in range(2):
            ring_copy(1, t, 0).start()

    @pl.when(jnp.logical_and(core == 1, jnp.logical_not(early)))
    def _():
        high_relays()

    loop(last_step - lag + 1, half_z, other_low)
    arrived(0, other, half_z, other)
    far_k, far_v = kv[0, 0, half_z, 0], kv[0, 1, half_z, 1]
    far_plane = plane_of(half_z, 1)
    flash(0, far_k, far_v, hidden(0, far_plane))

    def finish(g):
        for h in range(heads):
            r = pl.ds(g * rows + h * block, block)
            att[g, :, pl.ds(h * HEAD_SIZE, HEAD_SIZE)] = (
                acc[r, pl.ds(0, HEAD_SIZE)] / acc[r, pl.ds(HEAD_SIZE, HEAD_SIZE)]
            ).astype(BF16)

    def project(g, owner):
        return jnp.dot(
            att[g],
            wv[:, pl.ds(pl.multiple_of(owner * width, width), width)],
            preferred_element_type=F32,
        )

    def x_copy(g, d, o, p):
        return pltpu.make_async_remote_copy(
            src_ref=xs.at[g, d, o - 1, p],
            dst_ref=xr.at[g, d, o - 1, p],
            send_sem=xs_sem.at[g, d, o - 1, p],
            recv_sem=xr_sem.at[g, d, o - 1, p],
            device_id={"head": lax.rem(hx + (1, nx - 1)[d], nx)},
            device_id_type=MESH,
        )

    halves = (pl.ds(0, half), pl.ds(half, half))

    def reduce_stage(g, o):
        if o == half_x:
            own = project(g, lax.rem(hx + o, nx)).astype(BF16)
            for d in range(2):
                xs[g, d, o - 1, d] = own[:, d * half:(d + 1) * half]
                x_copy(g, d, o, d).start()
            return
        for d in range(2):
            own = project(g, lax.rem(hx + (o, nx - o)[d], nx))
            for p in (1 - d, d):
                term = own[:, p * half:(p + 1) * half]
                if o + 1 < half_x or p == d:
                    x_copy(g, d, o + 1, p).wait_recv()
                    term = term + xr[g, d, o, p].astype(F32)
                xs[g, d, o - 1, p] = term.astype(BF16)
                x_copy(g, d, o, p).start()

    def norm_copy(g, d):
        return pltpu.make_async_remote_copy(
            src_ref=ssq_out.at[g],
            dst_ref=ssq_in.at[g, d - 1],
            send_sem=n_send.at[g, d - 1],
            recv_sem=n_recv.at[g, d - 1],
            device_id={"head": lax.rem(hx + d, nx)},
            device_id_type=MESH,
        )

    def reduce_last(g):
        total = project(g, hx) + pick(g, res_ref, every).astype(F32)
        sides = []
        for p in range(2):
            side = total[:, p * half:(p + 1) * half]
            for d in (1 - p, p):
                x_copy(g, d, 1, p).wait_recv()
                side = side + xr[g, d, 0, p].astype(F32)
            mixed[g, :, halves[p]] = side
            sides.append(side)
        squares = sides[0] * sides[0] + sides[1] * sides[1]
        pieces = [squares[:, c * block:(c + 1) * block] for c in range(half // block)]
        column = functools.reduce(jnp.add, pieces)
        row = jnp.sum(column.T, axis=0, keepdims=True)
        ssq_out[g] = jnp.broadcast_to(row, ssq_out.shape[1:])
        for d in range(1, nx):
            norm_copy(g, d).start()

    def normalize(g):
        total = ssq_out[g]
        for d in range(1, nx):
            norm_copy(g, d).wait_recv()
            total = total + ssq_in[g, d - 1]
        inverse = lax.rsqrt(total / (nx * width) + NORM_EPSILON)
        column = jnp.broadcast_to(inverse[0:1, :], (block, block)).T
        for c in range(width // block):
            cols = pl.ds(c * block, block)
            mixed[g, :, cols] = mixed[g, :, cols] * column

    finish(0)
    loads[5].wait()
    loads[4].wait()
    reduce_stage(0, half_x)
    flash(1, far_k, far_v, None)

    def high_step(s, last):
        @pl.when(jnp.logical_and(core == 1, early))
        def _():
            relay(1, s, last)

        flash(1, both(0, 0, s), both(0, 1, s), None)
        for t in range(2):
            arrived(1, t, s, other)
        flash(
            1, both(1, 0, s), both(1, 1, s),
            hidden(1, plane_of(s, -1)) + hidden(1, plane_of(s, 1)),
        )

    cuts = [1 + (last_step - 1) * i // half_x for i in range(half_x + 1)]
    for i in range(half_x):
        loop(cuts[i], cuts[i + 1], lambda s: high_step(s, False))
        if half_x - 1 - i > 0:
            reduce_stage(0, half_x - 1 - i)
    high_step(last_step, True)

    @pl.when(jnp.logical_and(core == 1, early))
    def _():
        relay_far(1)

    arrived(1, other, half_z, other)
    flash(1, kv[1, 0, half_z, 0], kv[1, 1, half_z, 1], hidden(1, far_plane))
    finish(1)
    reduce_stage(1, half_x)
    reduce_last(0)
    for o in range(half_x - 1, 0, -1):
        reduce_stage(1, o)
    normalize(0)
    reduce_last(1)
    normalize(1)
    for g in range(2):
        for c in range(width // block):
            cols = pl.ds(c * block, block)
            low, high = mixed[0, :, cols], mixed[1, :, cols]
            out_ref[pl.ds(g * block, block), cols] = lax.select_n(
                swapped, *((low, high) if g == 0 else (high, low))
            )

    for g in range(2):
        for t in range(2):
            pair_copy(g, t).wait_send()
            ring_copy(g, t, 0).wait_send()
            share_copy(g, t, last_step).wait_send()
        ring_copy(g, mine, last_step).wait_send()
        share_copy(g, mine, half_z).wait_send()
        for d in range(1, nx):
            norm_copy(g, d).wait_send()
        for d in range(2):
            for o in range(1, half_x + 1):
                for p in range(2):
                    if o < half_x or p == d:
                        x_copy(g, d, o, p).wait_send()

    def drain(s):
        for g in range(2):
            for t in range(2):
                ring_copy(g, t, s).wait_send()
                share_copy(g, t, s).wait_send()

    loop(1, last_step, drain)


def body(queries, keys, values, residual, out_weight, norm_gain, block_order):
    nz = lax.axis_size("seq") // 2
    nx = lax.axis_size("head")
    tokens, q_width = queries.shape
    block = tokens // 2
    heads = q_width // HEAD_SIZE
    width = residual.shape[1]
    rows = heads * block
    half_z, half_x = nz // 2, nx // 2
    vmem = pl.BlockSpec(memory_space=pltpu.VMEM)
    hbm = pl.BlockSpec(memory_space=pltpu.HBM)
    dma = pltpu.SemaphoreType.DMA
    result = pl.pallas_call(
        functools.partial(kernel, (nz, nx, heads, block)),
        out_shape=jax.ShapeDtypeStruct((tokens, width), F32),
        in_specs=[hbm] * 6,
        out_specs=vmem,
        scratch_shapes=[
            pltpu.SMEM(block_order.shape, jnp.int32),
            pltpu.VMEM(queries.shape, BF16),
            pltpu.VMEM(keys.shape, BF16),
            pltpu.VMEM(values.shape, BF16),
            pltpu.VMEM(residual.shape, BF16),
            pltpu.VMEM(out_weight.shape, BF16),
            pltpu.VMEM((2 * rows, HEAD_SIZE), BF16),
            pltpu.VMEM((2, 2, half_z + 1, 2, tokens, HEAD_SIZE), BF16),
            pltpu.VMEM((2 * rows, 2 * HEAD_SIZE), F32),
            pltpu.VMEM((2 * rows, block), F32),
            pltpu.VMEM((2, block, q_width), BF16),
            pltpu.VMEM((2, 2, half_x, 2, block, width // 2), BF16),
            pltpu.VMEM((2, 2, half_x, 2, block, width // 2), BF16),
            pltpu.VMEM((2, block, width), F32),
            pltpu.VMEM((2, 8, block), F32),
            pltpu.VMEM((2, nx - 1, 8, block), F32),
            dma((6,)),
            dma((2, 2)),
            dma((2, 2)),
            dma((2, 2, half_z)),
            dma((2, 2, half_z + 1, 2)),
            dma((2, 2, half_z + 1)),
            dma((2, 2, half_x, 2)),
            dma((2, 2, half_x, 2)),
            dma((2, nx - 1)),
            dma((2, nx - 1)),
        ],
        compiler_params=pltpu.CompilerParams(
            collective_id=0, has_side_effects=True, vmem_limit_bytes=40 * 1024 * 1024
        ),
    )(block_order, queries, keys, values, residual, out_weight)
    return (result * norm_gain.astype(F32)[None, :]).astype(BF16)


def solution(mesh):
    split = P(("rep", "seq"), "head")
    return jax.shard_map(
        body,
        mesh=mesh,
        in_specs=(split, split, split, split, P("head", None), P("head"), P("rep")),
        out_specs=split,
        check_vma=False,
    )
```

time: 115 us -> 124 us (1.078)
  Pallas kernels: 105 us -> 116 us
  local copies, waits for them, and re-layouts: 8.42 us -> 6.42 us
    pallas_call x1, Pallas kernels: 105 us -> 116 us  [body(): pl.pallas_call(functools.partial(kernel, (nz, nx, heads, block)), out_sha...]
    convert_element_type x0 -> x2, other arithmetic: none -> 1.42 us  [body(): return (result * norm_gain.astype(F32)[None, :]).astype(BF16)]
where the time goes in v2:
time: 124 us
  Pallas kernels  116 us (94%)
  local copies, waits for them, and re-layouts  6.42 us (5%)
  other arithmetic  1.42 us (1%)
    pallas_call x1, Pallas kernels, body(): pl.pallas_call(functools.partial(kernel, (nz, nx, heads, block)), out_sha...  116 us
    unnamed x12, local copies, waits for them, and re-layouts  6.42 us

profile of v2, /device:TPU:80, one launch (start us, length us, event | category | flops | bytes accessed | tf_op | source)
XLA Modules:
  0.0 124.2 jit_solution(13170911510506018756)
XLA Ops:
  0.0 0.7 convert_element_type.6
  0.7 0.0 copy-start
  0.7 2.2 %copy-done = bf16[512,4096]{1,0:T(8,128)(2,1)S(1)} copy-done((bf16[512,4096]{1,0:T(8,128)(2,1)S(1)}, bf16[512,4096]{1,0:T(8,128)(2,1)}, u32[]{:S(2)}) %copy-start) | copy-done | bytes 4194328
  2.9 0.0 copy-start.1
  2.9 0.9 copy-done.1
  3.8 0.0 copy-start.2
  3.8 0.9 copy-done.2
  4.8 0.0 copy-start.3
  4.8 0.8 copy-done.3
  5.6 0.0 copy-start.4
  5.6 0.8 copy-done.4
  6.5 0.0 copy-start.5
  6.5 0.7 copy-done.5
  7.1 116.3 %shard_map.73 = f32[256,512]{1,0:T(8,128)S(1)} custom-call(s32[64]{0:T(128)S(1)} %copy-done.5, bf16[256,512]{1,0:T(8,128)(2,1)S(1)} %copy-done.1, bf16[256,128]{1,0:T(8,128)(2,1)S(1)} %copy-done.3, bf16[256,128]{1,0:T(8,128)(2,1)S(1)} %copy-done.4, bf16[256,512]{1,0:T(8,128)(2,1)S(1)} %copy-done.2, bf16[512,4096]{1,0:T(8,128)(2,1)S(1)} %copy-done), custom_call_target="tpu_custom_call" | custom-call | tf_op jit(solution)/shard_map/pallas_call | solution.py:443
  123.4 0.7 multiply_convert_fusion
Async XLA Ops:
  0.7 2.2 %copy-start = (bf16[512,4096]{1,0:T(8,128)(2,1)S(1)}, bf16[512,4096]{1,0:T(8,128)(2,1)}, u32[]{:S(2)}) copy-start(bf16[512,4096]{1,0:T(8,128)(2,1)} %w_hbm.1) | copy-start | bytes 12582916
  2.9 0.9 copy-start.1
  3.8 0.9 copy-start.2
  4.8 0.8 copy-start.3
  5.6 0.8 copy-start.4
  6.5 0.7 copy-start.5
